TPU v7x, 256 devices: a whole 4x4x8 slice. The times are simulated.
256 devices in a mesh: lat: 8 (over x, core), lon: 32 (over z, y).
Axes of the slice: x: 4, y: 4, z: 8, core: 2. Of those that a mesh axis runs over, the one named last changes fastest.
Arguments:
- grid: bfloat16 [720, 1440, 384], P('lat', 'lon'), may hold values from -33 to 33
- legendre: bfloat16 [384, 720, 384], P('lon', 'lat'), may hold values from -0.021606041 to 0.021606041, as said below
Outputs:
- normalized: bfloat16 [384, 384, 2, 384], P('lat', 'lon')
- spread: float32 [384], P('lat')
Inputs may be any that keep to these rules, and one draw needn't show every extreme that they name: legendre[m, j, l] is zero wherever l < m.
All inputs are finite; a program needn't handle non-finite values.
Results may differ from a plain program's by a relative error of at most 0.014.
Values may be sent and summed in bfloat16 or wider, within the bound.
A program may use at most 64 MiB of HBM per device.

v0:
```python
import math

import jax
import jax.numpy as jnp
from jax import lax
from jax.sharding import PartitionSpec as P

NLON = 1440
DEG = 384
CHANNELS = 64
MEMBERS = 6


epsilon = 1e-06


def copy_for_each(x, axis):
    copies = jnp.broadcast_to(x, (lax.axis_size(axis), *x.shape))
    return lax.all_to_all(copies, axis, split_axis=0, concat_axis=0, tiled=True)


def taken_together(x, axis):
    return copy_for_each(x, axis).sum(axis=0)


def spectral_table(order_ids):
    longitude = jnp.arange(NLON, dtype=jnp.int32)[:, None]
    phase = longitude * order_ids[None, :] % NLON
    angle = phase.astype(jnp.float32) * (2.0 * math.pi / NLON)
    stacked = jnp.stack([jnp.cos(angle), -jnp.sin(angle)], axis=1)
    return stacked.astype(jnp.bfloat16)


def legendre_terms(spectral, weights):
    groups, lat_rows, field_rows, parts, order_rows = spectral.shape
    product = jnp.einsum("sjfri,ijl->lirsf", spectral, weights, preferred_element_type=jnp.float32)
    return product.reshape(weights.shape[2], order_rows, parts, groups * field_rows)


def shards(grid, legendre):
    groups = lax.axis_size("lon")
    bands = lax.axis_size("lat")
    lat_rows, lon_rows, fields = grid.shape
    field_rows = fields // groups
    order_rows = DEG // groups
    degree_rows = DEG // bands
    pieces = jnp.transpose(grid.reshape(lat_rows, lon_rows, groups, field_rows), (2, 0, 1, 3))
    pieces = pieces.reshape(groups, lat_rows, lon_rows * field_rows)
    gathered = lax.all_to_all(pieces, "lon", split_axis=0, concat_axis=0, tiled=True).reshape(
        groups, lat_rows, lon_rows, field_rows
    )
    order_ids = jnp.arange(DEG, dtype=jnp.int32)
    basis = spectral_table(order_ids).reshape(groups, lon_rows, 2, groups, order_rows)
    spectrum = jnp.einsum("sjkf,skrgi->gjfri", gathered, basis, preferred_element_type=jnp.float32)
    spectrum = spectrum.astype(jnp.bfloat16).reshape(groups, lat_rows, field_rows * 2 * order_rows)
    spectral = lax.all_to_all(spectrum, "lon", split_axis=0, concat_axis=0, tiled=True)
    spectral = spectral.reshape(groups, lat_rows, field_rows, 2, order_rows)
    band_index = lax.axis_index("lat")
    degree_ids = band_index * degree_rows + jnp.arange(degree_rows, dtype=jnp.int32)
    partial_value = legendre_terms(spectral, legendre)
    summed = lax.psum(partial_value.astype(jnp.bfloat16), "lat").astype(jnp.float32)
    coeffs = lax.dynamic_slice_in_dim(summed, band_index * degree_rows, degree_rows, 0)
    by_member = coeffs.reshape(degree_rows, order_rows, 2, MEMBERS, CHANNELS)
    deviation = by_member - jnp.mean(by_member, axis=3, keepdims=True)
    squares = jnp.sum(deviation * deviation, axis=(1, 2, 3, 4))
    summed_squares = taken_together(squares, "lon")
    degree = degree_ids.astype(jnp.float32)
    spread = summed_squares / ((MEMBERS - 1) * CHANNELS * (2.0 * degree + 1.0))
    normalized = (coeffs * lax.rsqrt(spread + epsilon)[:, None, None, None]).astype(jnp.bfloat16)
    return (normalized, spread)


def solution(mesh):
    return jax.shard_map(
        shards,
        mesh=mesh,
        in_specs=(P("lat", "lon", None), P("lon", "lat", None)),
        out_specs=(P("lat", "lon", None, None), P("lat")),
        check_vma=False,
    )
```

profile of v0, /device:TPU:1, one launch (start us, length us, event | category | flops | bytes accessed | tf_op | source)
XLA Modules:
  0.0 380.1 jit_solution(15708152660878368889)
XLA Ops:
  7.2 0.0 copy-start
  7.2 7.0 %copy.53 = bf16[90,45,384]{0,1,2:T(8,128)(2,1)} copy(bf16[90,45,384]{2,1,0:T(8,128)(2,1)} %param.2) | data formatting | bytes 6220800 | tf_op args[0]
  14.2 7.3 %copy.54 = bf16[32,90,45,12]{1,0,3,2:T(8,128)(2,1)} copy(bf16[32,90,45,12]{1,2,3,0:T(8,128)(2,1)} %bitcast.39) | data formatting | bytes 6220800 | tf_op jit(solution)/shard_map/transpose | solution.py:47
  21.5 9.0 %copy.55 = bf16[32,90,540]{2,1,0:T(8,128)(2,1)} copy(bf16[32,90,540]{1,0,2:T(8,128)(2,1)} %bitcast.40) | data formatting | bytes 6220800 | tf_op jit(solution)/shard_map/reshape | solution.py:48
  30.5 12.1 %all-to-all-start = ((bf16[32,90,540]{2,1,0:T(8,128)(2,1)}), bf16[32,90,540]{2,1,0:T(8,128)(2,1)}, u32[]{:S(2)}, u32[]{:S(2)}) async-start(bf16[32,90,540]{2,1,0:T(8,128)(2,1)} %copy.55), calls=%async_computation | async-start | bytes 7864320 | tf_op jit(solution)/shard_map/all_to_all | solution.py:49
  42.6 0.2 all-reduce.2.cloned.1.call-start
  42.9 28.3 %cosine_convert_fusion = (bf16[32,45,1,32,12]{1,3,0,4,2:T(8,128)(2,1)}, bf16[32,45,1,32,12]{1,3,0,4,2:T(8,128)(2,1)}) fusion(s32[32,12]{0,1:T(8,128)S(1)} %multiply_add_fusion.1, s32[32,45]{1,0:T(8,128)S(1)} %multiply_add_fusion), kind=kLoop, calls=%fused_computation.9 | loop fusion | flops 6635520 | bytes 2219136 | tf_op jit(solution)/shard_map/convert
  71.2 58.6 %all-to-all-done = bf16[32,90,540]{2,1,0:T(8,128)(2,1)} async-done(((bf16[32,90,540]{2,1,0:T(8,128)(2,1)}), bf16[32,90,540]{2,1,0:T(8,128)(2,1)}, u32[]{:S(2)}, u32[]{:S(2)}) %all-to-all-start) | async-done | bytes 3110432 | tf_op jit(solution)/shard_map/all_to_all | solution.py:49
  129.7 8.2 %copy.56 = bf16[32,90,540]{1,0,2:T(8,128)(2,1)} copy(bf16[32,90,540]{2,1,0:T(8,128)(2,1)} %all-to-all-done) | data formatting | bytes 6220800 | tf_op jit(solution)/shard_map/all_to_all | solution.py:49
  137.9 12.0 %fusion.9 = bf16[32,90,12,2,12]{1,0,2,4,3:T(8,128)(2,1)S(1)} fusion(bf16[32,90,45,12,1,1]{1,0,3,2,5,4:T(8,128)(2,1)} %bitcast.43, bf16[32,45,1,32,12]{1,3,0,4,2:T(8,128)(2,1)} %get-tuple-element.15, bf16[32,45,1,32,12]{1,3,0,4,2:T(8,128)(2,1)} %get-tuple-element.14), kind=kOutput, calls=%fused_computation.16 | convolution fusion | flops 2394040320 | bytes 6981120 | tf_op jit(solution)/shard_map/sjkf,skrgi->gjfri/dot_general | solution.py:54
  149.9 0.6 copy.58
  150.5 0.9 copy.59
  151.4 64.7 %all_to_all.16 = bf16[32,90,288]{1,2,0:T(8,128)(2,1)S(1)} all-to-all(bf16[32,90,288]{1,2,0:T(8,128)(2,1)S(1)} %copy.59), channel_id=1, replica_groups=mesh['lat'=8,'lon'=32] {'lon'}, dimensions={0} | all-to-all | bytes 3317760 | tf_op jit(solution)/shard_map/all_to_all | solution.py:56
  216.2 0.9 copy.60
  217.1 0.0 copy-done
  217.1 2.2 convert_bitcast_fusion
  219.3 4.7 %copy.62 = bf16[384,12,2,32,12]{0,2,4,3,1:T(2,128)(2,1)} copy(bf16[384,12,2,32,12]{0,3,2,4,1:T(8,128)(2,1)S(1)} %convert_bitcast_fusion) | data formatting | bytes 14155776 | tf_op jit(solution)/shard_map/convert_element_type | solution.py:61
  224.0 17.8 %copy.63 = bf16[384,12,2,384]{3,0,2,1:T(8,128)(2,1)} copy(bf16[384,12,2,384]{0,2,3,1:T(2,128)(2,1)} %bitcast.38) | data formatting | bytes 14155776 | tf_op jit(solution)/shard_map/convert_element_type | solution.py:61
  241.8 0.0 all-reduce.2.cloned.1.call-update
  241.9 93.6 %all-reduce.2.cloned.1.call-done = bf16[384,12,2,384]{3,0,2,1:T(8,128)(2,1)} async-done(((bf16[384,12,2,384]{3,0,2,1:T(8,128)(2,1)}), bf16[384,12,2,384]{3,0,2,1:T(8,128)(2,1)}) %all-reduce.2.cloned.1.call-update) | async-done | bytes 7077904 | tf_op jit(solution)/shard_map/psum | solution.py:61
  335.4 1.3 dynamic-slice_convert_fusion
  336.8 3.0 reshape.108
  339.8 3.8 %reduce_sum.27 = f32[48,12,2,64]{3,0,2,1:T(8,128)S(1)} reduce(f32[48,12,2,6,64]{4,3,0,2,1:T(8,128)} %reshape.108, f32[]{:T(128)} %constant.38.clone.1), dimensions={3}, to_apply=%region_1.2 | reduce | flops 368640 | bytes 2064388 | tf_op jit(solution)/shard_map/reduce_sum | solution.py:64
  343.6 0.1 broadcast_multiply_fusion
  343.7 2.8 sub.11
  346.4 3.6 sub.12
  350.1 1.5 multiply_reduce_fusion
  351.6 18.0 %all_to_all.17 = f32[32,1,48]{2,1,0:T(1,128)S(1)} all-to-all(f32[32,1,48]{2,1,0:T(1,128)S(1)} %broadcast_in_dim.2), channel_id=1, replica_groups=mesh['lat'=8,'lon'=32] {'lon'}, dimensions={0} | all-to-all | bytes 12288 | tf_op jit(solution)/shard_map/all_to_all | solution.py:19
  369.6 0.5 add_rsqrt_fusion
  370.1 1.5 multiply_convert_fusion
  371.6 1.6 copy.65
  (4 shorter events, 0.1 us)
Async XLA Ops:
  7.2 209.9 %copy-start = (bf16[12,90,384]{2,1,0:T(8,128)(2,1)S(1)}, bf16[12,90,384]{2,1,0:T(8,128)(2,1)}, u32[]{:S(2)}) copy-start(bf16[12,90,384]{2,1,0:T(8,128)(2,1)} %param.3) | copy-start | bytes 2488324
  30.5 99.3 %all-to-all-start = ((bf16[32,90,540]{2,1,0:T(8,128)(2,1)}), bf16[32,90,540]{2,1,0:T(8,128)(2,1)}, u32[]{:S(2)}, u32[]{:S(2)}) async-start(bf16[32,90,540]{2,1,0:T(8,128)(2,1)} %copy.55), calls=%async_computation | async-start | bytes 7864320 | tf_op jit(solution)/shard_map/all_to_all | solution.py:49
  42.6 292.8 %all-reduce.2.cloned.1.call-start = ((), (), s32[]{:S(2)}) async-start(), calls=%async_computation.3 | async-start | bytes 14155776 | tf_op jit(solution)/shard_map/psum | solution.py:61
Sparse Core Ops, SparseCore 0:
  242.0 93.3 all-reduce.1
where the time goes:
time: 381 us; the launch traced here: 380 us
  waiting for transfers between devices  152 us (40%)
  blocking collectives  82.7 us (22%)
  local copies, waits for them, and re-layouts  67.5 us (18%)
  other arithmetic  37.1 us (10%)
  matrix products  14.1 us (4%)
  between operations  14.1 us (4%)
  starting transfers between devices  12.4 us (3%)
    psum x1, waiting for transfers between devices, shards(): lax.psum(partial_value.astype(jnp.bfloat16), 'lat').astype(jnp.float32)  93.6 us
    all_to_all x1, blocking collectives, shards(): lax.all_to_all(spectrum, 'lon', split_axis=0, concat_axis=0, tiled=True)  64.7 us
    all_to_all x1, waiting for transfers between devices, shards(): lax.all_to_all(pieces, 'lon', split_axis=0, concat_axis=0, tiled=True)  58.6 us
    another operation x1, other arithmetic  28.3 us
    convert_element_type x2, local copies, waits for them, and re-layouts, shards(): partial_value.astype(jnp.bfloat16)  22.6 us
    all_to_all x1, blocking collectives, copy_for_each(): return lax.all_to_all(copies, axis, split_axis=0, concat_axis=0, tiled=True)  18 us
    all_to_all x1, starting transfers between devices, shards(): lax.all_to_all(pieces, 'lon', split_axis=0, concat_axis=0, tiled=True)  12.1 us
    dot_general x1, matrix products, shards(): jnp.einsum('sjkf,skrgi->gjfri', gathered, basis, preferred_element_type=j...  12 us
  transfers between devices with their start and end apart: 2, of which 2 were waited for; matrix products, arithmetic and copies ran while one was open for 7% of the time, Pallas kernels for 0%

commit v1 on v0

v1 whole, which is shorter than its diff:
```python
import math

import jax
import jax.numpy as jnp
import numpy as np
from jax import lax
from jax.experimental import pallas as pl
from jax.experimental.pallas import tpu as pltpu
from jax.sharding import PartitionSpec as P

NLON = 1440
DEG = 384
CHANNELS = 64
MEMBERS = 6
FIELDS = 384
LAT = 8
LON = 32
ROWS = 90
LON_ROWS = 45
PADDED = 48
ORDERS = 12
DEGREES = 48
UNITS = 3
CHUNKS = 3
JPAD = 96
EPSILON = 1e-06
MESH = pl.DeviceIdType.MESH


def spectral_table():
    k = np.arange(NLON, dtype=np.int64)[:, None]
    m = np.arange(DEG, dtype=np.int64)[None, :]
    angle = ((k * m) % NLON).astype(np.float32) * np.float32(2.0 * math.pi / NLON)
    table = np.stack([np.cos(angle), -np.sin(angle)], axis=2).astype(np.float32)
    table = table.reshape(LON, LON_ROWS, LON, LAT, UNITS)
    padded = np.zeros((LON, PADDED, LON, LAT, UNITS), np.float32)
    padded[:, :LON_ROWS] = table
    return padded.transpose(3, 2, 4, 0, 1).reshape(2 * DEG, LON * PADDED).astype(jnp.bfloat16)


def wait_bytes(ref, sem):
    pltpu.make_async_copy(ref, ref, sem).wait()


def swap_matrix(major, minor):
    size = major * minor
    out_row = lax.broadcasted_iota(jnp.int32, (size, size), 0)
    in_row = lax.broadcasted_iota(jnp.int32, (size, size), 1)
    wanted = (out_row % major) * minor + out_row // major
    return (in_row == wanted).astype(jnp.float32).astype(jnp.bfloat16)


def kernel(
    grid_ref,
    leg_ref,
    basis_ref,
    out_ref,
    spread_ref,
    recv,
    basis,
    spec,
    mixed,
    sent,
    spectral,
    leg_raw,
    leg,
    part,
    coeffs,
    squares,
    all_squares,
    swap_spec,
    swap_leg,
    swap_out,
    basis_sem,
    grid_send,
    grid_recv,
    leg_send,
    leg_recv,
    mix_send,
    mix_recv,
    spec_send,
    spec_recv,
    coef_send,
    coef_recv,
    sq_send,
    sq_recv,
):
    b = lax.axis_index("lat")
    g = lax.axis_index("lon")

    def lon_peer(i):
        return (g + i) % LON

    def lat_peer(i):
        return (b + i) % LAT

    def has_row(chunk, d):
        return (chunk < 2) | (d % 5 != 4)

    def row_of(chunk, d):
        return chunk * LON + d - jnp.where(chunk == 2, d // 5, 0)

    basis_copy = pltpu.make_async_copy(basis_ref, basis, basis_sem)
    basis_copy.start()
    barrier = pltpu.get_barrier_semaphore()

    @pl.loop(1, LON)
    def _(i):
        pl.semaphore_signal(barrier, inc=1, device_id={"lon": lon_peer(i)}, device_id_type=MESH)

    @pl.loop(1, LAT)
    def _(i):
        pl.semaphore_signal(barrier, inc=1, device_id={"lat": lat_peer(i)}, device_id_type=MESH)

    pl.semaphore_wait(barrier, LON + LAT - 2)

    @pl.loop(1, LAT)
    def _(i):
        u = lat_peer(i)
        pltpu.make_async_remote_copy(
            src_ref=leg_ref.at[pl.ds(UNITS * u // 2, 2)],
            dst_ref=leg_raw.at[b],
            send_sem=leg_send,
            recv_sem=leg_recv,
            device_id={"lat": u},
            device_id_type=MESH,
        ).start()

    pltpu.make_async_copy(leg_ref.at[pl.ds(UNITS * b // 2, 2)], leg_raw.at[b], leg_recv).start()

    @pl.loop(0, CHUNKS)
    def _(chunk):
        @pl.loop(1, LON)
        def _(i):
            d = lon_peer(i)

            @pl.when(has_row(chunk, d))
            def _():
                pltpu.make_async_remote_copy(
                    src_ref=grid_ref.at[row_of(chunk, d)],
                    dst_ref=recv.at[chunk, g],
                    send_sem=grid_send.at[chunk],
                    recv_sem=grid_recv.at[chunk],
                    device_id={"lon": d},
                    device_id_type=MESH,
                ).start()

        @pl.when(has_row(chunk, g))
        def _():
            pltpu.make_async_copy(grid_ref.at[row_of(chunk, g)], recv.at[chunk, g], grid_recv.at[chunk]).start()

    swap_spec[...] = swap_matrix(LAT, 32)
    swap_leg[...] = swap_matrix(LAT, 16)
    swap_out[...] = swap_matrix(2 * ORDERS, 16)
    spectral[:, ROWS:] = jnp.zeros((UNITS, JPAD - ROWS, LAT, FIELDS), spectral.dtype)

    wait_bytes(leg_raw, leg_recv)
    for which in range(2):
        for block in range(JPAD // 16):
            first = 16 * block
            rows = min(16, ROWS - first)
            piece = leg_raw[:, which, first : first + rows, :].astype(jnp.float32)
            if rows < 16:
                piece = jnp.concatenate([piece, jnp.zeros((LAT, 16 - rows, DEG), jnp.float32)], axis=1)
            piece = piece.reshape(LAT * 16, DEG).astype(jnp.bfloat16)
            moved = jnp.dot(swap_leg[...], piece, preferred_element_type=jnp.float32)
            leg[which, :, 128 * block : 128 * (block + 1)] = moved.T.astype(jnp.bfloat16)

    basis_copy.wait()

    @pl.loop(0, CHUNKS)
    def _(chunk):
        @pl.when(has_row(chunk, g))
        def _():
            wait_bytes(recv.at[chunk], grid_recv.at[chunk])
            values = recv[chunk].reshape(LON * PADDED, FIELDS)
            rows = jnp.dot(basis[...], values, preferred_element_type=jnp.float32)
            spec[chunk] = rows.astype(jnp.bfloat16).reshape(LAT, LON * UNITS, FIELDS)

            @pl.loop(1, LAT)
            def _(i):
                u = lat_peer(i)
                pltpu.make_async_remote_copy(
                    src_ref=spec.at[chunk, u],
                    dst_ref=mixed.at[chunk, b],
                    send_sem=mix_send.at[chunk],
                    recv_sem=mix_recv.at[chunk],
                    device_id={"lat": u},
                    device_id_type=MESH,
                ).start()

            pltpu.make_async_copy(spec.at[chunk, b], mixed.at[chunk, b], mix_recv.at[chunk]).start()
            wait_bytes(mixed.at[chunk], mix_recv.at[chunk])
            for block in range(3):
                piece = mixed[chunk, :, 32 * block : 32 * (block + 1), :].reshape(LAT * 32, FIELDS)
                moved = jnp.dot(swap_spec[...], piece, preferred_element_type=jnp.float32)
                sent[chunk, 32 * block : 32 * (block + 1)] = moved.reshape(32, LAT, FIELDS).astype(jnp.bfloat16)
            row = row_of(chunk, g)

            @pl.loop(1, LON)
            def _(i):
                d = lon_peer(i)
                pltpu.make_async_remote_copy(
                    src_ref=sent.at[chunk, pl.ds(UNITS * d, UNITS)],
                    dst_ref=spectral.at[:, row],
                    send_sem=spec_send.at[chunk],
                    recv_sem=spec_recv,
                    device_id={"lon": d},
                    device_id_type=MESH,
                ).start()

            pltpu.make_async_copy(sent.at[chunk, pl.ds(UNITS * g, UNITS)], spectral.at[:, row], spec_recv).start()

    wait_bytes(spectral.at[:, pl.ds(0, ROWS)], spec_recv)
    for unit in range(UNITS):
        which = (UNITS * b + unit) // 2 - UNITS * b // 2
        values = spectral[unit].astype(jnp.float32).reshape(JPAD * LAT, FIELDS).astype(jnp.bfloat16)
        total = jnp.dot(leg[which], values, preferred_element_type=jnp.float32)
        part[:, unit] = total.astype(jnp.bfloat16).reshape(LAT, DEGREES, FIELDS)

    @pl.loop(1, LAT)
    def _(i):
        u = lat_peer(i)
        pltpu.make_async_remote_copy(
            src_ref=part.at[u],
            dst_ref=coeffs.at[b],
            send_sem=coef_send,
            recv_sem=coef_recv,
            device_id={"lat": u},
            device_id_type=MESH,
        ).start()

    pltpu.make_async_copy(part.at[b], coeffs.at[b], coef_recv).start()
    wait_bytes(coeffs, coef_recv)

    acc = jnp.zeros((128, 128), jnp.float32)
    total = jnp.zeros((DEGREES, 128), jnp.float32)
    for u in range(LAT):
        for unit in range(UNITS):
            x = coeffs[u, unit].astype(jnp.float32)
            tiles = [x[:, 128 * t : 128 * (t + 1)] for t in range(3)]
            both = tiles[0] + tiles[1] + tiles[2]
            mean = (both + pltpu.roll(both, CHANNELS, 1)) * (1.0 / MEMBERS)
            for tile in tiles:
                deviation = tile - mean
                total = total + deviation * deviation
    acc = jnp.concatenate([total, jnp.zeros((128 - DEGREES, 128), jnp.float32)], axis=0)
    squares[...] = jnp.broadcast_to(jnp.sum(acc.T, axis=0, keepdims=True), (8, 128))

    @pl.loop(1, LON)
    def _(i):
        d = lon_peer(i)
        pltpu.make_async_remote_copy(
            src_ref=squares,
            dst_ref=all_squares.at[g],
            send_sem=sq_send,
            recv_sem=sq_recv,
            device_id={"lon": d},
            device_id_type=MESH,
        ).start()

    pltpu.make_async_copy(squares, all_squares.at[g], sq_recv).start()
    wait_bytes(all_squares, sq_recv)
    summed = all_squares[0]
    for i in range(1, LON):
        summed = summed + all_squares[i]
    degree = (b * DEGREES + lax.broadcasted_iota(jnp.int32, (8, 128), 1)).astype(jnp.float32)
    spread = summed / ((MEMBERS - 1) * CHANNELS * (2.0 * degree + 1.0))
    spread_ref[...] = spread
    scale = lax.rsqrt(spread + EPSILON)
    scale = jnp.broadcast_to(scale[0:1], (128, 128)).T
    for block in range(3):
        rows = scale[16 * block : 16 * (block + 1)]
        rows = jnp.concatenate([rows, rows, rows], axis=1)
        x = coeffs[:, :, 16 * block : 16 * (block + 1), :].reshape(2 * ORDERS, 16, FIELDS).astype(jnp.float32)
        y = (x * rows[None]).astype(jnp.bfloat16).reshape(2 * ORDERS * 16, FIELDS)
        moved = jnp.dot(swap_out[...], y, preferred_element_type=jnp.float32)
        out_ref[16 * block : 16 * (block + 1)] = moved.reshape(16, 2 * ORDERS, FIELDS).astype(jnp.bfloat16)

    for chunk in range(CHUNKS):
        if chunk < 2:
            wait_bytes(recv.at[chunk, pl.ds(0, LON - 1)], grid_send.at[chunk])
        else:

            @pl.when(has_row(chunk, g))
            def _():
                wait_bytes(recv.at[chunk, pl.ds(0, 25)], grid_send.at[chunk])

            @pl.when(jnp.logical_not(has_row(chunk, g)))
            def _():
                wait_bytes(recv.at[chunk, pl.ds(0, 26)], grid_send.at[chunk])

        @pl.when(has_row(chunk, g))
        def _():
            wait_bytes(mixed.at[chunk, pl.ds(0, LAT - 1)], mix_send.at[chunk])
            wait_bytes(sent.at[chunk, pl.ds(0, UNITS * (LON - 1))], spec_send.at[chunk])

    wait_bytes(leg_raw.at[pl.ds(0, LAT - 1)], leg_send)
    wait_bytes(coeffs.at[pl.ds(0, LAT - 1)], coef_send)
    wait_bytes(all_squares.at[pl.ds(0, LON - 1)], sq_send)


def shards(grid, legendre):
    padded = jnp.pad(grid, ((0, 0), (0, PADDED - LON_ROWS), (0, 0)))
    basis = jnp.asarray(spectral_table())
    dma = pltpu.SemaphoreType.DMA
    bf16, f32 = jnp.bfloat16, jnp.float32
    any_space = pl.BlockSpec(memory_space=pl.ANY)
    vmem = pl.BlockSpec(memory_space=pltpu.VMEM)
    normalized, spread = pl.pallas_call(
        kernel,
        out_shape=(
            jax.ShapeDtypeStruct((DEGREES, 2 * ORDERS, FIELDS), bf16),
            jax.ShapeDtypeStruct((8, 128), f32),
        ),
        in_specs=[any_space, any_space, any_space],
        out_specs=(vmem, vmem),
        scratch_shapes=[
            pltpu.VMEM((CHUNKS, LON, PADDED, FIELDS), bf16),
            pltpu.VMEM((2 * DEG, LON * PADDED), bf16),
            pltpu.VMEM((CHUNKS, LAT, LON * UNITS, FIELDS), bf16),
            pltpu.VMEM((CHUNKS, LAT, LON * UNITS, FIELDS), bf16),
            pltpu.VMEM((CHUNKS, LON * UNITS, LAT, FIELDS), bf16),
            pltpu.VMEM((UNITS, JPAD, LAT, FIELDS), bf16),
            pltpu.VMEM((LAT, 2, ROWS, DEG), bf16),
            pltpu.VMEM((2, DEG, JPAD * LAT), bf16),
            pltpu.VMEM((LAT, UNITS, DEGREES, FIELDS), bf16),
            pltpu.VMEM((LAT, UNITS, DEGREES, FIELDS), bf16),
            pltpu.VMEM((8, 128), f32),
            pltpu.VMEM((LON, 8, 128), f32),
            pltpu.VMEM((256, 256), bf16),
            pltpu.VMEM((128, 128), bf16),
            pltpu.VMEM((384, 384), bf16),
            dma,
            dma((CHUNKS,)),
            dma((CHUNKS,)),
            dma,
            dma,
            dma((CHUNKS,)),
            dma((CHUNKS,)),
            dma((CHUNKS,)),
            dma,
            dma,
            dma,
            dma,
            dma,
        ],
        compiler_params=pltpu.CompilerParams(
            collective_id=0, has_side_effects=True, vmem_limit_bytes=48 * 1024 * 1024
        ),
        cost_estimate=pl.CostEstimate(flops=4_000_000_000, bytes_accessed=8_000_000, transcendentals=0),
    )(padded, legendre, basis)
    return normalized.reshape(DEGREES, ORDERS, 2, FIELDS), spread[0, :DEGREES]


def solution(mesh):
    return jax.shard_map(
        shards,
        mesh=mesh,
        in_specs=(P("lat", "lon", None), P("lon", "lat", None)),
        out_specs=(P("lat", "lon", None, None), P("lat")),
        check_vma=False,
    )
```

time: 381 us -> 150 us (0.39)
  waiting for transfers between devices: 152 us -> 0 us
  Pallas kernels: 0 us -> 143 us
  blocking collectives: 82.7 us -> 0 us
  local copies, waits for them, and re-layouts: 67.5 us -> 5.88 us
  other arithmetic: 37.1 us -> 0 us
  matrix products: 14.1 us -> 0 us
  between operations: 14.1 us -> 0.66 us
  starting transfers between devices: 12.4 us -> 0 us
    pallas_call x0 -> x1, Pallas kernels: none -> 143 us  [shards(): pl.pallas_call(kernel, out_shape=(jax.ShapeDtypeStruct((DEGREES, 2 * ORDE...]
    psum x1 -> x0, waiting for transfers between devices: 93.6 us -> none  [shards(): lax.psum(partial_value.astype(jnp.bfloat16), 'lat').astype(jnp.float32)]
    all_to_all x2 -> x0, blocking collectives: 82.7 us -> none  [the longest x1 64.7 us: shards(): lax.all_to_all(spectrum, 'lon', split_axis=0, concat_axis=0, tiled=True)]
    all_to_all x1 -> x0, waiting for transfers between devices: 58.6 us -> none  [shards(): lax.all_to_all(pieces, 'lon', split_axis=0, concat_axis=0, tiled=True)]
    another operation x1 -> x0, other arithmetic: 28.3 us -> none
    convert_element_type x3 -> x0, local copies, waits for them, and re-layouts: 23.2 us -> none  [the longest x2 22.6 us: shards(): partial_value.astype(jnp.bfloat16)]
    dot_general x2 -> x0, matrix products: 14.1 us -> none  [the longest x1 12 us: shards(): jnp.einsum('sjkf,skrgi->gjfri', gathered, basis, preferred_element_type=j...]
    all_to_all x1 -> x0, starting transfers between devices: 12.1 us -> none  [shards(): lax.all_to_all(pieces, 'lon', split_axis=0, concat_axis=0, tiled=True)]
  transfers between devices with their start and end apart: 2 -> 0, of which waited for: 2 -> 0; matrix products, arithmetic and copies ran while one was open for 7% -> 0% of each run, Pallas kernels for 0% -> 0%
where the time goes in v1:
time: 150 us
  Pallas kernels  143 us (95%)
  local copies, waits for them, and re-layouts  5.88 us (4%)
    pallas_call x1, Pallas kernels, shards(): pl.pallas_call(kernel, out_shape=(jax.ShapeDtypeStruct((DEGREES, 2 * ORDE...  143 us
    pad x1, local copies, waits for them, and re-layouts, shards(): padded = jnp.pad(grid, ((0, 0), (0, PADDED - LON_ROWS), (0, 0)))  4.12 us

profile of v1, /device:TPU:1, one launch (start us, length us, event | category | flops | bytes accessed | tf_op | source)
XLA Modules:
  0.0 149.8 jit_solution(9463133728446491930)
XLA Ops:
  0.6 0.0 copy-start.1
  0.6 0.0 copy-start
  0.7 4.1 %pad.4.grid_ref = bf16[90,48,384]{2,1,0:T(8,128)(2,1)} pad(bf16[90,45,384]{2,1,0:T(8,128)(2,1)} %param.3, bf16[]{:T(256)} %constant.4.clone.1), padding=0_0x0_3x0_0 | pad | bytes 6428162 | tf_op jit(solution)/shard_map/jit(_pad)/pad | solution.py:304
  4.8 0.0 copy-done.1
  4.8 0.0 copy-done
  4.8 143.2 %shard_map.50 = (bf16[48,24,384]{2,1,0:T(8,128)(2,1)S(1)}, f32[8,128]{1,0:T(8,128)S(1)}) custom-call(bf16[90,48,384]{2,1,0:T(8,128)(2,1)} %pad.4.grid_ref, bf16[12,90,384]{2,1,0:T(8,128)(2,1)S(1)} %copy-done, bf16[768,1536]{1,0:T(8,128)(2,1)S(1)} %copy-done.1), custom_call_target="tpu_custom_call" | custom-call | flops 4000000000 | bytes 8000000 | tf_op jit(solution)/shard_map/pallas_call | solution.py:310
  148.0 1.2 reshape.7
  149.2 0.5 slice_bitcast_fusion
Async XLA Ops:
  0.6 4.1 %copy-start.1 = (bf16[768,1536]{1,0:T(8,128)(2,1)S(1)}, bf16[768,1536]{1,0:T(8,128)(2,1)}, u32[]{:S(2)}) copy-start(bf16[768,1536]{1,0:T(8,128)(2,1)} %constant.5.clone.basis_ref) | copy-start | bytes 7077892
  0.6 4.1 %copy-start = (bf16[12,90,384]{2,1,0:T(8,128)(2,1)S(1)}, bf16[12,90,384]{2,1,0:T(8,128)(2,1)}, u32[]{:S(2)}) copy-start(bf16[12,90,384]{2,1,0:T(8,128)(2,1)} %leg_ref.1) | copy-start | bytes 2488324

commit v2 on v1

v2 whole, which is shorter than its diff:
```python
import math

import jax
import jax.numpy as jnp
import numpy as np
from jax import lax
from jax.experimental import pallas as pl
from jax.experimental.pallas import tpu as pltpu
from jax.sharding import PartitionSpec as P

NLON = 1440
DEG = 384
CHANNELS = 64
MEMBERS = 6
FIELDS = 384
LAT = 8
LON = 32
ROWS = 90
LON_ROWS = 45
MAIN = 40
REST = LON_ROWS - MAIN
REST_PAD = 16
ORDERS = 12
DEGREES = 48
UNITS = 3
CHUNKS = 3
JPAD = 96
EPSILON = 1e-06
MESH = pl.DeviceIdType.MESH


def spectral_table():
    k = np.arange(NLON, dtype=np.int64)[:, None]
    m = np.arange(DEG, dtype=np.int64)[None, :]
    angle = ((k * m) % NLON).astype(np.float32) * np.float32(2.0 * math.pi / NLON)
    table = np.stack([np.cos(angle), -np.sin(angle)], axis=2).astype(np.float32)
    table = table.reshape(LON, LON_ROWS, LON, LAT, UNITS)
    table = table.transpose(3, 2, 4, 0, 1).reshape(2 * DEG, LON, LON_ROWS)
    rest = np.zeros((2 * DEG, LON, REST_PAD), np.float32)
    rest[:, :, :REST] = table[:, :, MAIN:]
    main = table[:, :, :MAIN].reshape(2 * DEG, LON * MAIN)
    return main.astype(jnp.bfloat16), rest.reshape(2 * DEG, LON * REST_PAD).astype(jnp.bfloat16)


def wait_bytes(ref, sem):
    pltpu.make_async_copy(ref, ref, sem).wait()


def swap_matrix(major, minor):
    size = major * minor
    out_row = lax.broadcasted_iota(jnp.int32, (size, size), 0)
    in_row = lax.broadcasted_iota(jnp.int32, (size, size), 1)
    wanted = (out_row % major) * minor + out_row // major
    return (in_row == wanted).astype(jnp.float32).astype(jnp.bfloat16)


def kernel(
    grid_ref,
    leg_ref,
    main_ref,
    rest_ref,
    out_ref,
    spread_ref,
    recv,
    rest_raw,
    rest_out,
    rest_in,
    basis,
    rest_basis,
    spec,
    mixed,
    sent,
    spectral,
    leg_raw,
    leg,
    begun,
    part,
    coeffs,
    turned,
    squares,
    all_squares,
    swap_spec,
    swap_leg,
    swap_out,
    basis_sem,
    raw_sem,
    grid_send,
    grid_recv,
    rest_send,
    rest_recv,
    leg_send,
    leg_recv,
    mix_send,
    mix_recv,
    spec_send,
    spec_recv,
    last_recv,
    coef_send,
    coef_recv,
    sq_send,
    sq_recv,
):
    b = lax.axis_index("lat")
    g = lax.axis_index("lon")

    def lon_peer(i):
        return (g + i) % LON

    def lat_peer(i):
        return (b + i) % LAT

    def has_row(chunk, d):
        return (chunk < 2) | (d % 5 != 4)

    def row_of(chunk, d):
        return chunk * LON + d - jnp.where(chunk == 2, d // 5, 0)

    def to_lon(src, dst, send_sem, recv_sem, d):
        pltpu.make_async_remote_copy(
            src_ref=src, dst_ref=dst, send_sem=send_sem, recv_sem=recv_sem, device_id={"lon": d}, device_id_type=MESH
        ).start()

    def to_lat(src, dst, send_sem, recv_sem, d):
        pltpu.make_async_remote_copy(
            src_ref=src, dst_ref=dst, send_sem=send_sem, recv_sem=recv_sem, device_id={"lat": d}, device_id_type=MESH
        ).start()

    raw_copy = pltpu.make_async_copy(grid_ref.at[:, pl.ds(MAIN, REST)], rest_raw, raw_sem)
    raw_copy.start()
    basis_copy = pltpu.make_async_copy(main_ref, basis, basis_sem.at[0])
    basis_copy.start()
    first_rest_copy = pltpu.make_async_copy(rest_ref, rest_basis.at[0], basis_sem.at[1])
    first_rest_copy.start()
    barrier = pltpu.get_barrier_semaphore()

    @pl.loop(1, LON)
    def _(i):
        pl.semaphore_signal(barrier, inc=1, device_id={"lon": lon_peer(i)}, device_id_type=MESH)

    @pl.loop(1, LAT)
    def _(i):
        pl.semaphore_signal(barrier, inc=1, device_id={"lat": lat_peer(i)}, device_id_type=MESH)

    raw_copy.wait()

    @pl.loop(0, LON)
    def _(d):
        pieces = [rest_raw[row_of(chunk, d)].astype(jnp.float32) for chunk in range(2)]
        last = rest_raw[jnp.minimum(row_of(2, d), ROWS - 1)].astype(jnp.float32)
        pieces += [jnp.where(has_row(2, d), last, 0.0), jnp.zeros((1, FIELDS), jnp.float32)]
        rest_out[d] = jnp.concatenate(pieces, axis=0).astype(jnp.bfloat16)

    pl.semaphore_wait(barrier, LON + LAT - 2)

    @pl.loop(1, LAT)
    def _(i):
        u = lat_peer(i)
        to_lat(leg_ref.at[pl.ds(UNITS * u // 2, 2)], leg_raw.at[b], leg_send, leg_recv, u)

    pltpu.make_async_copy(leg_ref.at[pl.ds(UNITS * b // 2, 2)], leg_raw.at[b], leg_recv).start()

    @pl.loop(1, LON)
    def _(i):
        d = lon_peer(i)
        to_lon(rest_out.at[d], rest_in.at[g], rest_send, rest_recv, d)

    pltpu.make_async_copy(rest_out.at[g], rest_in.at[g], rest_recv).start()

    @pl.loop(0, CHUNKS)
    def _(chunk):
        @pl.loop(1, LON)
        def _(i):
            d = lon_peer(i)

            @pl.when(has_row(chunk, d))
            def _():
                src = grid_ref.at[row_of(chunk, d), pl.ds(0, MAIN)]
                to_lon(src, recv.at[chunk, g], grid_send.at[chunk], grid_recv.at[chunk], d)

        @pl.when(has_row(chunk, g))
        def _():
            src = grid_ref.at[row_of(chunk, g), pl.ds(0, MAIN)]
            pltpu.make_async_copy(src, recv.at[chunk, g], grid_recv.at[chunk]).start()

    swap_spec[...] = swap_matrix(LAT, 32)
    swap_leg[...] = swap_matrix(LAT, 16)
    swap_out[...] = swap_matrix(2 * ORDERS, 16)
    spectral[:, ROWS:] = jnp.zeros((UNITS, JPAD - ROWS, LAT, FIELDS), spectral.dtype)

    first_rest_copy.wait()
    size = LON * REST_PAD
    from_column = lax.broadcasted_iota(jnp.int32, (size, size), 0)
    to_column = lax.broadcasted_iota(jnp.int32, (size, size), 1)
    for chunk in range(1, CHUNKS):
        move = (from_column + REST * chunk == to_column).astype(jnp.float32).astype(jnp.bfloat16)
        moved = jnp.dot(rest_basis[0], move, preferred_element_type=jnp.float32)
        rest_basis[chunk] = moved.astype(jnp.bfloat16)

    wait_bytes(leg_raw, leg_recv)
    for which in range(2):
        for block in range(JPAD // 16):
            first = 16 * block
            rows = min(16, ROWS - first)
            piece = leg_raw[:, which, first : first + rows, :].astype(jnp.float32)
            if rows < 16:
                piece = jnp.concatenate([piece, jnp.zeros((LAT, 16 - rows, DEG), jnp.float32)], axis=1)
            piece = piece.reshape(LAT * 16, DEG).astype(jnp.bfloat16)
            moved = jnp.dot(swap_leg[...], piece, preferred_element_type=jnp.float32)
            leg[which, :, 128 * block : 128 * (block + 1)] = moved.T.astype(jnp.bfloat16)

    def send_spectrum(chunk):
        row = row_of(chunk, g)

        @pl.loop(1, LON)
        def _(i):
            d = lon_peer(i)
            src = sent.at[chunk, pl.ds(UNITS * d, UNITS)]
            to_lon(src, spectral.at[:, row], spec_send.at[chunk], spec_recv, d)

        pltpu.make_async_copy(sent.at[chunk, pl.ds(UNITS * g, UNITS)], spectral.at[:, row], spec_recv).start()

    def send_last():
        row = row_of(2, g)
        for unit in range(UNITS):

            @pl.loop(1, LON)
            def _(i):
                d = lon_peer(i)
                src = sent.at[2, UNITS * d + unit]
                to_lon(src, spectral.at[unit, row], spec_send.at[2], last_recv.at[unit], d)

            pltpu.make_async_copy(sent.at[2, UNITS * g + unit], spectral.at[unit, row], last_recv.at[unit]).start()

    basis_copy.wait()
    wait_bytes(rest_in, rest_recv)

    @pl.loop(0, CHUNKS)
    def _(chunk):
        @pl.when(has_row(chunk, g))
        def _():
            wait_bytes(recv.at[chunk], grid_recv.at[chunk])
            values = recv[chunk].astype(jnp.float32).reshape(LON * MAIN, FIELDS).astype(jnp.bfloat16)
            rows = jnp.dot(basis[...], values, preferred_element_type=jnp.float32)
            values = rest_in[...].reshape(LON * REST_PAD, FIELDS)
            rows = rows + jnp.dot(rest_basis[chunk], values, preferred_element_type=jnp.float32)
            spec[chunk] = rows.astype(jnp.bfloat16).reshape(LAT, LON * UNITS, FIELDS)

            @pl.loop(1, LAT)
            def _(i):
                u = lat_peer(i)
                to_lat(spec.at[chunk, u], mixed.at[chunk, b], mix_send.at[chunk], mix_recv.at[chunk], u)

            pltpu.make_async_copy(spec.at[chunk, b], mixed.at[chunk, b], mix_recv.at[chunk]).start()
            wait_bytes(mixed.at[chunk], mix_recv.at[chunk])
            for block in range(3):
                piece = mixed[chunk, :, 32 * block : 32 * (block + 1), :].reshape(LAT * 32, FIELDS)
                moved = jnp.dot(swap_spec[...], piece, preferred_element_type=jnp.float32)
                sent[chunk, 32 * block : 32 * (block + 1)] = moved.reshape(32, LAT, FIELDS).astype(jnp.bfloat16)
            pl.when(chunk < 2)(lambda: send_spectrum(chunk))
            pl.when(chunk == 2)(send_last)

    early = 2 * LON
    wait_bytes(spectral.at[:, pl.ds(0, early)], spec_recv)

    def table_of(unit):
        return (UNITS * b + unit) // 2 - UNITS * b // 2

    for unit in range(UNITS):
        values = spectral[unit, :early].astype(jnp.float32).reshape(early * LAT, FIELDS).astype(jnp.bfloat16)
        begun[unit] = jnp.dot(leg[table_of(unit), :, : early * LAT], values, preferred_element_type=jnp.float32)
    for unit in range(UNITS):
        wait_bytes(spectral.at[unit, pl.ds(early, ROWS - early)], last_recv.at[unit])
        values = spectral[unit, early:].astype(jnp.float32).reshape((JPAD - early) * LAT, FIELDS).astype(jnp.bfloat16)
        total = jnp.dot(leg[table_of(unit), :, early * LAT :], values, preferred_element_type=jnp.float32)
        total = begun[unit] + total
        part[:, unit] = total.astype(jnp.bfloat16).reshape(LAT, DEGREES, FIELDS)

        @pl.loop(1, LAT)
        def _(i):
            u = lat_peer(i)
            to_lat(part.at[u, unit], coeffs.at[b, unit], coef_send, coef_recv.at[unit], u)

        pltpu.make_async_copy(part.at[b, unit], coeffs.at[b, unit], coef_recv.at[unit]).start()

    total = jnp.zeros((DEGREES, 128), jnp.float32)
    for unit in range(UNITS):
        wait_bytes(coeffs.at[:, unit], coef_recv.at[unit])
        for u in range(LAT):
            x = coeffs[u, unit].astype(jnp.float32)
            tiles = [x[:, 128 * t : 128 * (t + 1)] for t in range(3)]
            both = tiles[0] + tiles[1] + tiles[2]
            mean = (both + pltpu.roll(both, CHANNELS, 1)) * (1.0 / MEMBERS)
            for tile in tiles:
                deviation = tile - mean
                total = total + deviation * deviation
    acc = jnp.concatenate([total, jnp.zeros((128 - DEGREES, 128), jnp.float32)], axis=0)
    squares[...] = jnp.sum(acc.T, axis=0, keepdims=True)

    @pl.loop(1, LON)
    def _(i):
        to_lon(squares, all_squares.at[g], sq_send, sq_recv, lon_peer(i))

    pltpu.make_async_copy(squares, all_squares.at[g], sq_recv).start()
    for block in range(3):
        x = coeffs[:, :, 16 * block : 16 * (block + 1), :].reshape(2 * ORDERS * 16, FIELDS)
        moved = jnp.dot(swap_out[...], x, preferred_element_type=jnp.float32)
        turned[16 * block : 16 * (block + 1)] = moved.reshape(16, 2 * ORDERS, FIELDS)

    wait_bytes(all_squares, sq_recv)
    summed = all_squares[0]
    for i in range(1, LON):
        summed = summed + all_squares[i]
    degree = (b * DEGREES + lax.broadcasted_iota(jnp.int32, (1, 128), 1)).astype(jnp.float32)
    spread = summed / ((MEMBERS - 1) * CHANNELS * (2.0 * degree + 1.0))
    spread_ref[...] = jnp.broadcast_to(spread, (8, 128))
    scale = jnp.broadcast_to(lax.rsqrt(spread + EPSILON), (128, 128)).T
    scale = jnp.concatenate([scale[:DEGREES]] * 3, axis=1)
    for degree in range(DEGREES):
        out_ref[degree] = (turned[degree] * scale[degree : degree + 1]).astype(jnp.bfloat16)

    for chunk in range(CHUNKS):
        if chunk < 2:
            wait_bytes(recv.at[chunk, pl.ds(0, LON - 1)], grid_send.at[chunk])
        else:

            @pl.when(has_row(chunk, g))
            def _():
                wait_bytes(recv.at[chunk, pl.ds(0, 25)], grid_send.at[chunk])

            @pl.when(jnp.logical_not(has_row(chunk, g)))
            def _():
                wait_bytes(recv.at[chunk, pl.ds(0, 26)], grid_send.at[chunk])

        @pl.when(has_row(chunk, g))
        def _():
            wait_bytes(mixed.at[chunk, pl.ds(0, LAT - 1)], mix_send.at[chunk])
            wait_bytes(sent.at[chunk, pl.ds(0, UNITS * (LON - 1))], spec_send.at[chunk])

    wait_bytes(rest_in.at[pl.ds(0, LON - 1)], rest_send)
    wait_bytes(leg_raw.at[pl.ds(0, LAT - 1)], leg_send)
    wait_bytes(coeffs.at[pl.ds(0, LAT - 1)], coef_send)
    wait_bytes(all_squares.at[pl.ds(0, LON - 1)], sq_send)


def shards(grid, legendre):
    main, rest = [jnp.asarray(table) for table in spectral_table()]
    dma = pltpu.SemaphoreType.DMA
    bf16, f32 = jnp.bfloat16, jnp.float32
    any_space = pl.BlockSpec(memory_space=pl.ANY)
    vmem = pl.BlockSpec(memory_space=pltpu.VMEM)
    normalized, spread = pl.pallas_call(
        kernel,
        out_shape=(
            jax.ShapeDtypeStruct((DEGREES, 2 * ORDERS, FIELDS), bf16),
            jax.ShapeDtypeStruct((8, 128), f32),
        ),
        in_specs=[any_space] * 4,
        out_specs=(vmem, vmem),
        scratch_shapes=[
            pltpu.VMEM((CHUNKS, LON, MAIN, FIELDS), bf16),
            pltpu.VMEM((ROWS, REST, FIELDS), bf16),
            pltpu.VMEM((LON, REST_PAD, FIELDS), bf16),
            pltpu.VMEM((LON, REST_PAD, FIELDS), bf16),
            pltpu.VMEM((2 * DEG, LON * MAIN), bf16),
            pltpu.VMEM((CHUNKS, 2 * DEG, LON * REST_PAD), bf16),
            pltpu.VMEM((CHUNKS, LAT, LON * UNITS, FIELDS), bf16),
            pltpu.VMEM((CHUNKS, LAT, LON * UNITS, FIELDS), bf16),
            pltpu.VMEM((CHUNKS, LON * UNITS, LAT, FIELDS), bf16),
            pltpu.VMEM((UNITS, JPAD, LAT, FIELDS), bf16),
            pltpu.VMEM((LAT, 2, ROWS, DEG), bf16),
            pltpu.VMEM((2, DEG, JPAD * LAT), bf16),
            pltpu.VMEM((UNITS, DEG, FIELDS), f32),
            pltpu.VMEM((LAT, UNITS, DEGREES, FIELDS), bf16),
            pltpu.VMEM((LAT, UNITS, DEGREES, FIELDS), bf16),
            pltpu.VMEM((DEGREES, 2 * ORDERS, FIELDS), f32),
            pltpu.VMEM((1, 128), f32),
            pltpu.VMEM((LON, 1, 128), f32),
            pltpu.VMEM((256, 256), bf16),
            pltpu.VMEM((128, 128), bf16),
            pltpu.VMEM((384, 384), bf16),
            dma((2,)),
            dma,
            dma((CHUNKS,)),
            dma((CHUNKS,)),
            dma,
            dma,
            dma,
            dma,
            dma((CHUNKS,)),
            dma((CHUNKS,)),
            dma((CHUNKS,)),
            dma,
            dma((UNITS,)),
            dma,
            dma((UNITS,)),
            dma,
            dma,
        ],
        compiler_params=pltpu.CompilerParams(
            collective_id=0, has_side_effects=True, vmem_limit_bytes=48 * 1024 * 1024
        ),
        cost_estimate=pl.CostEstimate(flops=4_000_000_000, bytes_accessed=8_000_000, transcendentals=0),
    )(*[pltpu.with_memory_space_constraint(x, pltpu.HBM) for x in (grid, legendre, main, rest)])
    return normalized.reshape(DEGREES, ORDERS, 2, FIELDS), spread[0, :DEGREES]


def solution(mesh):
    return jax.shard_map(
        shards,
        mesh=mesh,
        in_specs=(P("lat", "lon", None), P("lon", "lat", None)),
        out_specs=(P("lat", "lon", None, None), P("lat")),
        check_vma=False,
    )
```

time: 150 us -> 135 us (0.900)
  Pallas kernels: 143 us -> 133 us
  local copies, waits for them, and re-layouts: 5.88 us -> 1.75 us
    pallas_call x1, Pallas kernels: 143 us -> 133 us  [shards(): pl.pallas_call(kernel, out_shape=(jax.ShapeDtypeStruct((DEGREES, 2 * ORDE...]
    pad x1 -> x0, local copies, waits for them, and re-layouts: 4.12 us -> none  [shards(): padded = jnp.pad(grid, ((0, 0), (0, PADDED - LON_ROWS), (0, 0)))]
where the time goes in v2:
time: 135 us
  Pallas kernels  133 us (99%)
  local copies, waits for them, and re-layouts  1.75 us (1%)
    pallas_call x1, Pallas kernels, shards(): pl.pallas_call(kernel, out_shape=(jax.ShapeDtypeStruct((DEGREES, 2 * ORDE...  133 us

profile of v2, /device:TPU:1, one launch (start us, length us, event | category | flops | bytes accessed | tf_op | source)
XLA Modules:
  0.0 135.1 jit_solution(9316274265216532545)
XLA Ops:
  0.6 132.7 %shard_map.59 = (bf16[48,24,384]{2,1,0:T(8,128)(2,1)S(1)}, f32[8,128]{1,0:T(8,128)S(1)}) custom-call(bf16[90,45,384]{2,1,0:T(8,128)(2,1)} %grid_ref.1, bf16[12,90,384]{2,1,0:T(8,128)(2,1)} %leg_ref.1, bf16[768,1280]{1,0:T(8,128)(2,1)} %constant.4.clone.main_ref, bf16[768,512]{1,0:T(8,128)(2,1)} %constant.5.clone.rest_ref), custom_call_target="tpu_custom_call" | custom-call | flops 4000000000 | bytes 8000000 | tf_op jit(solution)/shard_map/pallas_call | solution.py:351
  133.3 1.2 reshape.7
  134.6 0.5 slice_bitcast_fusion

commit v3 on v2

--- a/solution.py
+++ b/solution.py
@@ -1,3 +1,4 @@
+import functools
 import math
 
 import jax
@@ -77,8 +78,11 @@
     part,
     coeffs,
     turned,
+    by_degree,
     squares,
     all_squares,
+    unit_squares,
+    all_units,
     swap_spec,
     swap_leg,
     swap_out,
@@ -99,6 +103,8 @@
     coef_recv,
     sq_send,
     sq_recv,
+    unit_send,
+    unit_recv,
 ):
     b = lax.axis_index("lat")
     g = lax.axis_index("lon")
@@ -109,11 +115,24 @@
     def lat_peer(i):
         return (b + i) % LAT
 
-    def has_row(chunk, d):
-        return (chunk < 2) | (d % 5 != 4)
-
-    def row_of(chunk, d):
-        return chunk * LON + d - jnp.where(chunk == 2, d // 5, 0)
+    def first_piece(d):
+        return 39 * d // 16
+
+    def has_piece(d, k):
+        return first_piece(d) + k < first_piece(d + 1)
+
+    def piece_of(d, k):
+        piece = first_piece(d) + k
+        return 2 * LON + piece // 3, pl.ds(pl.multiple_of(128 * (piece % 3), 128), 128)
+
+    def each_piece(d, action):
+        for k in range(CHUNKS):
+            row, fields = piece_of(d, k)
+            run = functools.partial(action, row, fields, pl.ds(128 * k, 128))
+            if k < 2:
+                run()
+            else:
+                pl.when(has_piece(d, k))(run)
 
     def to_lon(src, dst, send_sem, recv_sem, d):
         pltpu.make_async_remote_copy(
@@ -141,46 +160,67 @@
     def _(i):
         pl.semaphore_signal(barrier, inc=1, device_id={"lat": lat_peer(i)}, device_id_type=MESH)
 
-    raw_copy.wait()
-
-    @pl.loop(0, LON)
-    def _(d):
-        pieces = [rest_raw[row_of(chunk, d)].astype(jnp.float32) for chunk in range(2)]
-        last = rest_raw[jnp.minimum(row_of(2, d), ROWS - 1)].astype(jnp.float32)
-        pieces += [jnp.where(has_row(2, d), last, 0.0), jnp.zeros((1, FIELDS), jnp.float32)]
-        rest_out[d] = jnp.concatenate(pieces, axis=0).astype(jnp.bfloat16)
-
     pl.semaphore_wait(barrier, LON + LAT - 2)
 
-    @pl.loop(1, LAT)
-    def _(i):
-        u = lat_peer(i)
-        to_lat(leg_ref.at[pl.ds(UNITS * u // 2, 2)], leg_raw.at[b], leg_send, leg_recv, u)
-
-    pltpu.make_async_copy(leg_ref.at[pl.ds(UNITS * b // 2, 2)], leg_raw.at[b], leg_recv).start()
-
-    @pl.loop(1, LON)
-    def _(i):
-        d = lon_peer(i)
-        to_lon(rest_out.at[d], rest_in.at[g], rest_send, rest_recv, d)
-
-    pltpu.make_async_copy(rest_out.at[g], rest_in.at[g], rest_recv).start()
-
-    @pl.loop(0, CHUNKS)
-    def _(chunk):
+    def send_rows(chunk):
         @pl.loop(1, LON)
         def _(i):
             d = lon_peer(i)
-
-            @pl.when(has_row(chunk, d))
-            def _():
-                src = grid_ref.at[row_of(chunk, d), pl.ds(0, MAIN)]
-                to_lon(src, recv.at[chunk, g], grid_send.at[chunk], grid_recv.at[chunk], d)
-
-        @pl.when(has_row(chunk, g))
-        def _():
-            src = grid_ref.at[row_of(chunk, g), pl.ds(0, MAIN)]
-            pltpu.make_async_copy(src, recv.at[chunk, g], grid_recv.at[chunk]).start()
+            src = grid_ref.at[chunk * LON + d, pl.ds(0, MAIN)]
+            to_lon(src, recv.at[chunk, g], grid_send.at[chunk], grid_recv.at[chunk], d)
+
+        src = grid_ref.at[chunk * LON + g, pl.ds(0, MAIN)]
+        pltpu.make_async_copy(src, recv.at[chunk, g], grid_recv.at[chunk]).start()
+
+    send_rows(0)
+
+    @pl.loop(1, LAT)
+    def _(i):
+        u = lat_peer(i)
+        to_lat(leg_ref.at[pl.ds(UNITS * u // 2, 2)], leg_raw.at[b], leg_send, leg_recv, u)
+
+    pltpu.make_async_copy(leg_ref.at[pl.ds(UNITS * b // 2, 2)], leg_raw.at[b], leg_recv).start()
+
+    raw_copy.wait()
+
+    @pl.loop(0, LON)
+    def _(d):
+        pieces = [rest_raw[d].astype(jnp.float32), rest_raw[LON + d].astype(jnp.float32)]
+        last = []
+        for k in range(CHUNKS):
+            row, fields = piece_of(d, k)
+            last.append(rest_raw[row, :, fields].astype(jnp.float32))
+        last[2] = jnp.where(has_piece(d, 2), last[2], 0.0)
+        pieces += [jnp.concatenate(last, axis=1), jnp.zeros((1, FIELDS), jnp.float32)]
+        rest_out[d] = jnp.concatenate(pieces, axis=0).astype(jnp.bfloat16)
+
+    @pl.loop(1, LON)
+    def _(i):
+        d = lon_peer(i)
+        to_lon(rest_out.at[d], rest_in.at[g], rest_send, rest_recv, d)
+
+    pltpu.make_async_copy(rest_out.at[g], rest_in.at[g], rest_recv).start()
+    send_rows(1)
+
+    @pl.loop(1, LON)
+    def _(i):
+        d = lon_peer(i)
+
+        def send(row, fields, lanes):
+            src = grid_ref.at[row, pl.ds(0, MAIN), fields]
+            to_lon(src, recv.at[2, g, :, lanes], grid_send.at[2], grid_recv.at[2], d)
+
+        each_piece(d, send)
+
+    def keep(row, fields, lanes):
+        src = grid_ref.at[row, pl.ds(0, MAIN), fields]
+        pltpu.make_async_copy(src, recv.at[2, g, :, lanes], grid_recv.at[2]).start()
+
+    each_piece(g, keep)
+
+    @pl.when(jnp.logical_not(has_piece(g, 2)))
+    def _():
+        recv[2, :, :, 256:] = jnp.zeros((LON, MAIN, 128), recv.dtype)
 
     swap_spec[...] = swap_matrix(LAT, 32)
     swap_leg[...] = swap_matrix(LAT, 16)
@@ -209,7 +249,7 @@
             leg[which, :, 128 * block : 128 * (block + 1)] = moved.T.astype(jnp.bfloat16)
 
     def send_spectrum(chunk):
-        row = row_of(chunk, g)
+        row = chunk * LON + g
 
         @pl.loop(1, LON)
         def _(i):
@@ -220,44 +260,56 @@
         pltpu.make_async_copy(sent.at[chunk, pl.ds(UNITS * g, UNITS)], spectral.at[:, row], spec_recv).start()
 
     def send_last():
-        row = row_of(2, g)
         for unit in range(UNITS):
 
             @pl.loop(1, LON)
             def _(i):
                 d = lon_peer(i)
-                src = sent.at[2, UNITS * d + unit]
-                to_lon(src, spectral.at[unit, row], spec_send.at[2], last_recv.at[unit], d)
-
-            pltpu.make_async_copy(sent.at[2, UNITS * g + unit], spectral.at[unit, row], last_recv.at[unit]).start()
+
+                def send(row, fields, lanes):
+                    src = sent.at[2, UNITS * d + unit, :, lanes]
+                    to_lon(src, spectral.at[unit, row, :, fields], spec_send.at[2], last_recv.at[unit], d)
+
+                each_piece(g, send)
+
+            def keep(row, fields, lanes):
+                src = sent.at[2, UNITS * g + unit, :, lanes]
+                pltpu.make_async_copy(src, spectral.at[unit, row, :, fields], last_recv.at[unit]).start()
+
+            each_piece(g, keep)
 
     basis_copy.wait()
     wait_bytes(rest_in, rest_recv)
 
     @pl.loop(0, CHUNKS)
     def _(chunk):
-        @pl.when(has_row(chunk, g))
+        @pl.when((chunk < 2) | has_piece(g, 2))
         def _():
             wait_bytes(recv.at[chunk], grid_recv.at[chunk])
-            values = recv[chunk].astype(jnp.float32).reshape(LON * MAIN, FIELDS).astype(jnp.bfloat16)
-            rows = jnp.dot(basis[...], values, preferred_element_type=jnp.float32)
-            values = rest_in[...].reshape(LON * REST_PAD, FIELDS)
-            rows = rows + jnp.dot(rest_basis[chunk], values, preferred_element_type=jnp.float32)
-            spec[chunk] = rows.astype(jnp.bfloat16).reshape(LAT, LON * UNITS, FIELDS)
-
-            @pl.loop(1, LAT)
-            def _(i):
-                u = lat_peer(i)
-                to_lat(spec.at[chunk, u], mixed.at[chunk, b], mix_send.at[chunk], mix_recv.at[chunk], u)
-
-            pltpu.make_async_copy(spec.at[chunk, b], mixed.at[chunk, b], mix_recv.at[chunk]).start()
-            wait_bytes(mixed.at[chunk], mix_recv.at[chunk])
-            for block in range(3):
-                piece = mixed[chunk, :, 32 * block : 32 * (block + 1), :].reshape(LAT * 32, FIELDS)
-                moved = jnp.dot(swap_spec[...], piece, preferred_element_type=jnp.float32)
-                sent[chunk, 32 * block : 32 * (block + 1)] = moved.reshape(32, LAT, FIELDS).astype(jnp.bfloat16)
-            pl.when(chunk < 2)(lambda: send_spectrum(chunk))
-            pl.when(chunk == 2)(send_last)
+
+        @pl.when((chunk == 2) & jnp.logical_not(has_piece(g, 2)))
+        def _():
+            wait_bytes(recv.at[chunk, :, :, pl.ds(0, 256)], grid_recv.at[chunk])
+
+        values = recv[chunk].astype(jnp.float32).reshape(LON * MAIN, FIELDS).astype(jnp.bfloat16)
+        rows = jnp.dot(basis[...], values, preferred_element_type=jnp.float32)
+        values = rest_in[...].reshape(LON * REST_PAD, FIELDS)
+        rows = rows + jnp.dot(rest_basis[chunk], values, preferred_element_type=jnp.float32)
+        spec[chunk] = rows.astype(jnp.bfloat16).reshape(LAT, LON * UNITS, FIELDS)
+
+        @pl.loop(1, LAT)
+        def _(i):
+            u = lat_peer(i)
+            to_lat(spec.at[chunk, u], mixed.at[chunk, b], mix_send.at[chunk], mix_recv.at[chunk], u)
+
+        pltpu.make_async_copy(spec.at[chunk, b], mixed.at[chunk, b], mix_recv.at[chunk]).start()
+        wait_bytes(mixed.at[chunk], mix_recv.at[chunk])
+        for block in range(3):
+            piece = mixed[chunk, :, 32 * block : 32 * (block + 1), :].reshape(LAT * 32, FIELDS)
+            moved = jnp.dot(swap_spec[...], piece, preferred_element_type=jnp.float32)
+            sent[chunk, 32 * block : 32 * (block + 1)] = moved.reshape(32, LAT, FIELDS).astype(jnp.bfloat16)
+        pl.when(chunk < 2)(lambda: send_spectrum(chunk))
+        pl.when(chunk == 2)(send_last)
 
     early = 2 * LON
     wait_bytes(spectral.at[:, pl.ds(0, early)], spec_recv)
@@ -278,68 +330,77 @@
         @pl.loop(1, LAT)
         def _(i):
             u = lat_peer(i)
-            to_lat(part.at[u, unit], coeffs.at[b, unit], coef_send, coef_recv.at[unit], u)
-
-        pltpu.make_async_copy(part.at[b, unit], coeffs.at[b, unit], coef_recv.at[unit]).start()
-
-    total = jnp.zeros((DEGREES, 128), jnp.float32)
-    for unit in range(UNITS):
-        wait_bytes(coeffs.at[:, unit], coef_recv.at[unit])
-        for u in range(LAT):
-            x = coeffs[u, unit].astype(jnp.float32)
-            tiles = [x[:, 128 * t : 128 * (t + 1)] for t in range(3)]
-            both = tiles[0] + tiles[1] + tiles[2]
-            mean = (both + pltpu.roll(both, CHANNELS, 1)) * (1.0 / MEMBERS)
-            for tile in tiles:
-                deviation = tile - mean
-                total = total + deviation * deviation
-    acc = jnp.concatenate([total, jnp.zeros((128 - DEGREES, 128), jnp.float32)], axis=0)
-    squares[...] = jnp.sum(acc.T, axis=0, keepdims=True)
+            to_lat(part.at[u, unit], coeffs.at[b, unit], coef_send, coef_recv, u)
+
+        pltpu.make_async_copy(part.at[b, unit], coeffs.at[b, unit], coef_recv).start()
+        tiles = [total[:, 128 * t : 128 * (t + 1)] for t in range(3)]
+        both = tiles[0] + tiles[1] + tiles[2]
+        mean = (both + pltpu.roll(both, CHANNELS, 1)) * (1.0 / MEMBERS)
+        square = sum((tile - mean) * (tile - mean) for tile in tiles)
+        by_degree[...] = square if unit == 0 else by_degree[...] + square
+
+    for third in range(3):
+        rows = by_degree[128 * third : 128 * (third + 1)]
+        squares[third : third + 1] = jnp.sum(rows.T, axis=0, keepdims=True)
 
     @pl.loop(1, LON)
     def _(i):
         to_lon(squares, all_squares.at[g], sq_send, sq_recv, lon_peer(i))
 
     pltpu.make_async_copy(squares, all_squares.at[g], sq_recv).start()
+    wait_bytes(all_squares, sq_recv)
+    summed = all_squares[0]
+    for i in range(1, LON):
+        summed = summed + all_squares[i]
+    unit_squares[...] = summed
+
+    @pl.loop(1, LAT)
+    def _(i):
+        to_lat(unit_squares, all_units.at[b], unit_send, unit_recv, lat_peer(i))
+
+    pltpu.make_async_copy(unit_squares, all_units.at[b], unit_recv).start()
+    wait_bytes(coeffs, coef_recv)
     for block in range(3):
         x = coeffs[:, :, 16 * block : 16 * (block + 1), :].reshape(2 * ORDERS * 16, FIELDS)
         moved = jnp.dot(swap_out[...], x, preferred_element_type=jnp.float32)
         turned[16 * block : 16 * (block + 1)] = moved.reshape(16, 2 * ORDERS, FIELDS)
 
-    wait_bytes(all_squares, sq_recv)
-    summed = all_squares[0]
-    for i in range(1, LON):
-        summed = summed + all_squares[i]
-    degree = (b * DEGREES + lax.broadcasted_iota(jnp.int32, (1, 128), 1)).astype(jnp.float32)
-    spread = summed / ((MEMBERS - 1) * CHANNELS * (2.0 * degree + 1.0))
-    spread_ref[...] = jnp.broadcast_to(spread, (8, 128))
-    scale = jnp.broadcast_to(lax.rsqrt(spread + EPSILON), (128, 128)).T
-    scale = jnp.concatenate([scale[:DEGREES]] * 3, axis=1)
+    wait_bytes(all_units, unit_recv)
+    summed = all_units[0]
+    for i in range(1, LAT):
+        summed = summed + all_units[i]
+    for third in range(3):
+        by_degree[128 * third : 128 * (third + 1)] = jnp.broadcast_to(summed[third : third + 1], (128, 128)).T
+    first_degree = pl.multiple_of(b * DEGREES, DEGREES)
+    degree = (first_degree + lax.broadcasted_iota(jnp.int32, (DEGREES, 128), 0)).astype(jnp.float32)
+    spread = by_degree[pl.ds(first_degree, DEGREES)] / ((MEMBERS - 1) * CHANNELS * (2.0 * degree + 1.0))
+    square = jnp.concatenate([spread, jnp.zeros((128 - DEGREES, 128), jnp.float32)], axis=0)
+    spread_ref[...] = square.T[:8]
+    scale = jnp.concatenate([lax.rsqrt(spread + EPSILON)] * 3, axis=1)
     for degree in range(DEGREES):
         out_ref[degree] = (turned[degree] * scale[degree : degree + 1]).astype(jnp.bfloat16)
 
+    for chunk in range(2):
+        wait_bytes(recv.at[chunk, pl.ds(0, LON - 1)], grid_send.at[chunk])
+        wait_bytes(sent.at[chunk, pl.ds(0, UNITS * (LON - 1))], spec_send.at[chunk])
+
+    @pl.when(has_piece(g, 2))
+    def _():
+        wait_bytes(recv.at[2, pl.ds(0, 25)], grid_send.at[2])
+        wait_bytes(sent.at[2, pl.ds(0, UNITS * (LON - 1))], spec_send.at[2])
+
+    @pl.when(jnp.logical_not(has_piece(g, 2)))
+    def _():
+        wait_bytes(recv.at[pl.ds(0, 2), pl.ds(0, 19), :, pl.ds(0, 256)], grid_send.at[2])
+        wait_bytes(sent.at[2, pl.ds(0, UNITS * (LON - 1)), :, pl.ds(0, 256)], spec_send.at[2])
+
     for chunk in range(CHUNKS):
-        if chunk < 2:
-            wait_bytes(recv.at[chunk, pl.ds(0, LON - 1)], grid_send.at[chunk])
-        else:
-
-            @pl.when(has_row(chunk, g))
-            def _():
-                wait_bytes(recv.at[chunk, pl.ds(0, 25)], grid_send.at[chunk])
-
-            @pl.when(jnp.logical_not(has_row(chunk, g)))
-            def _():
-                wait_bytes(recv.at[chunk, pl.ds(0, 26)], grid_send.at[chunk])
-
-        @pl.when(has_row(chunk, g))
-        def _():
-            wait_bytes(mixed.at[chunk, pl.ds(0, LAT - 1)], mix_send.at[chunk])
-            wait_bytes(sent.at[chunk, pl.ds(0, UNITS * (LON - 1))], spec_send.at[chunk])
-
+        wait_bytes(mixed.at[chunk, pl.ds(0, LAT - 1)], mix_send.at[chunk])
     wait_bytes(rest_in.at[pl.ds(0, LON - 1)], rest_send)
     wait_bytes(leg_raw.at[pl.ds(0, LAT - 1)], leg_send)
     wait_bytes(coeffs.at[pl.ds(0, LAT - 1)], coef_send)
     wait_bytes(all_squares.at[pl.ds(0, LON - 1)], sq_send)
+    wait_bytes(all_units.at[pl.ds(0, LAT - 1)], unit_send)
 
 
 def shards(grid, legendre):
@@ -373,8 +434,11 @@
             pltpu.VMEM((LAT, UNITS, DEGREES, FIELDS), bf16),
             pltpu.VMEM((LAT, UNITS, DEGREES, FIELDS), bf16),
             pltpu.VMEM((DEGREES, 2 * ORDERS, FIELDS), f32),
-            pltpu.VMEM((1, 128), f32),
-            pltpu.VMEM((LON, 1, 128), f32),
+            pltpu.VMEM((DEG, 128), f32),
+            pltpu.VMEM((3, 128), f32),
+            pltpu.VMEM((LON, 3, 128), f32),
+            pltpu.VMEM((3, 128), f32),
+            pltpu.VMEM((LAT, 3, 128), f32),
             pltpu.VMEM((256, 256), bf16),
             pltpu.VMEM((128, 128), bf16),
             pltpu.VMEM((384, 384), bf16),
@@ -392,7 +456,9 @@
             dma,
             dma((UNITS,)),
             dma,
-            dma((UNITS,)),
+            dma,
+            dma,
+            dma,
             dma,
             dma,
         ],

time: 135 us -> 133 us (0.985)
  Pallas kernels: 133 us -> 131 us
    pallas_call x1, Pallas kernels: 133 us -> 131 us  [shards(): pl.pallas_call(kernel, out_shape=(jax.ShapeDtypeStruct((DEGREES, 2 * ORDE...]
where the time goes in v3:
time: 133 us
  Pallas kernels  131 us (98%)
  local copies, waits for them, and re-layouts  1.75 us (1%)
    pallas_call x1, Pallas kernels, shards(): pl.pallas_call(kernel, out_shape=(jax.ShapeDtypeStruct((DEGREES, 2 * ORDE...  131 us

profile of v3, /device:TPU:1, one launch (start us, length us, event | category | flops | bytes accessed | tf_op | source)
XLA Modules:
  0.0 133.0 jit_solution(7384010523477428324)
XLA Ops:
  0.6 130.6 %shard_map.59 = (bf16[48,24,384]{2,1,0:T(8,128)(2,1)S(1)}, f32[8,128]{1,0:T(8,128)S(1)}) custom-call(bf16[90,45,384]{2,1,0:T(8,128)(2,1)} %grid_ref.1, bf16[12,90,384]{2,1,0:T(8,128)(2,1)} %leg_ref.1, bf16[768,1280]{1,0:T(8,128)(2,1)} %constant.4.clone.main_ref, bf16[768,512]{1,0:T(8,128)(2,1)} %constant.5.clone.rest_ref), custom_call_target="tpu_custom_call" | custom-call | flops 4000000000 | bytes 8000000 | tf_op jit(solution)/shard_map/pallas_call | solution.py:412
  131.3 1.2 reshape.7
  132.5 0.5 slice_bitcast_fusion

commit v4 on v3

--- a/solution.py
+++ b/solution.py
@@ -28,6 +28,7 @@
 JPAD = 96
 EPSILON = 1e-06
 MESH = pl.DeviceIdType.MESH
+GROUPS = ((0, 2), (2, 1))
 
 
 def spectral_table():
@@ -260,21 +261,23 @@
         pltpu.make_async_copy(sent.at[chunk, pl.ds(UNITS * g, UNITS)], spectral.at[:, row], spec_recv).start()
 
     def send_last():
-        for unit in range(UNITS):
+        for part_id, (first, count) in enumerate(GROUPS):
 
             @pl.loop(1, LON)
             def _(i):
                 d = lon_peer(i)
 
                 def send(row, fields, lanes):
-                    src = sent.at[2, UNITS * d + unit, :, lanes]
-                    to_lon(src, spectral.at[unit, row, :, fields], spec_send.at[2], last_recv.at[unit], d)
+                    src = sent.at[2, pl.ds(UNITS * d + first, count), :, lanes]
+                    dst = spectral.at[pl.ds(first, count), row, :, fields]
+                    to_lon(src, dst, spec_send.at[2], last_recv.at[part_id], d)
 
                 each_piece(g, send)
 
             def keep(row, fields, lanes):
-                src = sent.at[2, UNITS * g + unit, :, lanes]
-                pltpu.make_async_copy(src, spectral.at[unit, row, :, fields], last_recv.at[unit]).start()
+                src = sent.at[2, pl.ds(UNITS * g + first, count), :, lanes]
+                dst = spectral.at[pl.ds(first, count), row, :, fields]
+                pltpu.make_async_copy(src, dst, last_recv.at[part_id]).start()
 
             each_piece(g, keep)
 
@@ -321,7 +324,9 @@
         values = spectral[unit, :early].astype(jnp.float32).reshape(early * LAT, FIELDS).astype(jnp.bfloat16)
         begun[unit] = jnp.dot(leg[table_of(unit), :, : early * LAT], values, preferred_element_type=jnp.float32)
     for unit in range(UNITS):
-        wait_bytes(spectral.at[unit, pl.ds(early, ROWS - early)], last_recv.at[unit])
+        for part_id, (first, count) in enumerate(GROUPS):
+            if first == unit:
+                wait_bytes(spectral.at[pl.ds(first, count), pl.ds(early, ROWS - early)], last_recv.at[part_id])
         values = spectral[unit, early:].astype(jnp.float32).reshape((JPAD - early) * LAT, FIELDS).astype(jnp.bfloat16)
         total = jnp.dot(leg[table_of(unit), :, early * LAT :], values, preferred_element_type=jnp.float32)
         total = begun[unit] + total

time: 133 us -> 133 us (level)
  no operation moved by 1% of the time
where the time goes in v4:
time: 133 us
  Pallas kernels  131 us (98%)
  local copies, waits for them, and re-layouts  1.75 us (1%)
    pallas_call x1, Pallas kernels, shards(): pl.pallas_call(kernel, out_shape=(jax.ShapeDtypeStruct((DEGREES, 2 * ORDE...  131 us

profile of v4, /device:TPU:1, one launch (start us, length us, event | category | flops | bytes accessed | tf_op | source)
XLA Modules:
  0.0 132.9 jit_solution(8900751022123011716)
XLA Ops:
  0.6 130.5 %shard_map.59 = (bf16[48,24,384]{2,1,0:T(8,128)(2,1)S(1)}, f32[8,128]{1,0:T(8,128)S(1)}) custom-call(bf16[90,45,384]{2,1,0:T(8,128)(2,1)} %grid_ref.1, bf16[12,90,384]{2,1,0:T(8,128)(2,1)} %leg_ref.1, bf16[768,1280]{1,0:T(8,128)(2,1)} %constant.4.clone.main_ref, bf16[768,512]{1,0:T(8,128)(2,1)} %constant.5.clone.rest_ref), custom_call_target="tpu_custom_call" | custom-call | flops 4000000000 | bytes 8000000 | tf_op jit(solution)/shard_map/pallas_call | solution.py:417
  131.2 1.2 reshape.7
  132.4 0.5 slice_bitcast_fusion
